TPU v7x, 32 devices: a whole 2x2x4 slice. The times are simulated.
32 devices in a mesh: layer: 4 (over y, x), row: 2 (over core), col: 4 (over z).
Axes of the slice: x: 2, y: 2, z: 4, core: 2. Of those that a mesh axis runs over, the one named last changes fastest.
Arguments:
- hidden: bfloat16 [384, 2304], P(('layer', 'row')), may hold values from -60 to 60
- embedding: bfloat16 [16384, 2304], P(('row', 'col'), 'layer'), may hold values from -0.3 to 0.3
- teacher: bfloat16 [384, 16384], P('layer', ('row', 'col')), may hold values from -80 to 240
Outputs:
- grad_embedding: float32 [16384, 2304], P(('row', 'col'), 'layer')
- grad_hidden: float32 [384, 2304], P(('layer', 'row', 'col'))
All inputs are finite; a program needn't handle non-finite values.
Results may differ from a plain program's by a relative error of at most 0.0041.
Values may be sent and summed in bfloat16 or wider, within the bound.
A program may use at most 192 MiB of HBM per device.

v0:
```python
import jax
import jax.numpy as jnp
from jax import lax
from jax.sharding import PartitionSpec as P

LOSS_SCALE = 256


def local(hidden, embedding, teacher):
    token_rows = lax.all_gather(hidden, "row", axis=0, tiled=True)
    width_part = lax.all_to_all(token_rows, "layer", split_axis=1, concat_axis=0, tiled=True)
    logits = lax.psum_scatter(
        lax.dot_general(
            width_part, embedding, (((1,), (1,)), ((), ())), preferred_element_type=jnp.float32
        ),
        "layer",
        scatter_dimension=0,
        tiled=True,
    )
    teach_f = teacher.astype(jnp.float32)
    top_s, top_t = lax.pmax((jnp.max(logits, axis=1), jnp.max(teach_f, axis=1)), ("row", "col"))
    part_s = jnp.sum(jnp.exp(logits - top_s[:, None]), axis=1)
    part_t = jnp.sum(jnp.exp(teach_f - top_t[:, None]), axis=1)
    sum_s, sum_t = lax.psum((part_s, part_t), ("row", "col"))
    lse_s = top_s + jnp.log(sum_s)
    lse_t = top_t + jnp.log(sum_t)
    prob_s = jnp.exp(logits - lse_s[:, None])
    prob_t = jnp.exp(teach_f - lse_t[:, None])
    grads = ((prob_s - prob_t) * LOSS_SCALE).astype(jnp.bfloat16)
    grad_piece = lax.all_gather(grads, "layer", axis=0, tiled=True)
    embed_acc = lax.dot_general(
        grad_piece, width_part, (((0,), (0,)), ((), ())), preferred_element_type=jnp.float32
    )
    hidden_piece = jnp.dot(grad_piece, embedding, preferred_element_type=jnp.float32)
    hidden_terms = lax.all_to_all(hidden_piece, "layer", split_axis=0, concat_axis=1, tiled=True)
    grad_hidden = lax.psum_scatter(hidden_terms, ("row", "col"), scatter_dimension=0, tiled=True)
    return (embed_acc, grad_hidden)


def solution(mesh):
    placed = (P(("layer", "row"), None), P(("row", "col"), "layer"), P("layer", ("row", "col")))
    return jax.shard_map(
        local,
        mesh=mesh,
        in_specs=placed,
        out_specs=(P(("row", "col"), "layer"), P(("layer", "row", "col"), None)),
        check_vma=False,
    )
```

profile of v0, /device:TPU:1, one launch (start us, length us, event | category | flops | bytes accessed | tf_op | source)
XLA Modules:
  0.0 216.0 jit_solution(10763876937868347929)
XLA Ops:
  7.2 2.5 %all_gather.6 = bf16[96,2304]{1,0:T(8,128)(2,1)S(1)} all-gather(bf16[48,2304]{1,0:T(8,128)(2,1)} %param.3), channel_id=1, replica_groups=mesh['layer'=4,'row'=2,'col'=4] {'row'}, dimensions={0}, use_global_device_ids=true | all-gather | bytes 663552 | tf_op jit(solution)/shard_map/all_gather | solution.py:10
  10.3 11.5 %all_to_all.38 = bf16[96,4,576]{2,0,1:T(8,128)(2,1)S(1)} all-to-all(bf16[96,4,576]{2,0,1:T(8,128)(2,1)S(1)} %copy.11), channel_id=1, replica_groups=mesh['layer'=4,'row'=2,'col'=4] {'layer'}, dimensions={1} | all-to-all | bytes 884736 | tf_op jit(solution)/shard_map/all_to_all | solution.py:11
  21.8 0.8 copy-done.2
  22.6 3.1 %fusion.7 = f32[384,2048]{1,0:T(8,128)} fusion(bf16[384,576]{1,0:T(8,128)(2,1)S(1)} %bitcast.14, bf16[2048,576]{0,1:T(8,128)(2,1)S(1)} %copy-done), kind=kOutput, calls=%fused_computation.12 | convolution fusion | flops 905969664 | bytes 5947392 | tf_op jit(solution)/shard_map/dot_general | solution.py:13
  25.8 0.9 copy-done.5
  26.8 43.8 %reduce-scatter.4.cloned.1.call-done = f32[96,2048]{1,0:T(8,128)} async-done(((f32[384,2048]{1,0:T(8,128)}), f32[96,2048]{1,0:T(8,128)}) %reduce-scatter.4.cloned.1.call-update) | async-done | bytes 786448 | tf_op jit(solution)/shard_map/reduce_scatter | solution.py:12
  70.6 1.3 reduce_max.23
  72.0 17.8 %all-reduce.3 = (f32[96]{0:T(128)S(1)}, f32[96]{0:T(128)S(1)}) all-reduce(bf16[96]{0:T(256)(128)(2,1)S(1)} %reduce_max.24, f32[96]{0:T(128)S(1)} %reduce_max.23), channel_id=1, replica_groups=mesh['layer'=4,'row'=2,'col'=4] {'row','col'}, use_global_device_ids=true, to_apply=%region_6.0 | all-reduce | flops 192 | bytes 1344 | tf_op jit(solution)/shard_map/pmax | solution.py:21
  89.8 1.5 fusion.2
  91.4 14.2 %all-reduce.2 = (f32[96]{0:T(128)}, f32[96]{0:T(128)}) all-reduce(f32[96]{0:T(128)S(1)} %get-tuple-element.6, f32[96]{0:T(128)S(1)} %get-tuple-element.7), channel_id=1, replica_groups=mesh['layer'=4,'row'=2,'col'=4] {'row','col'}, use_global_device_ids=true, to_apply=%region_8.0 | all-reduce | flops 192 | bytes 1536 | tf_op jit(solution)/shard_map/psum | solution.py:24
  106.9 1.1 fusion.6
  108.0 29.8 %all-gather.2.cloned.1.call-done = bf16[384,2048]{1,0:T(8,128)(2,1)} async-done(((bf16[96,2048]{1,0:T(8,128)(2,1)}), bf16[384,2048]{1,0:T(8,128)(2,1)}) %all-gather.2.cloned.1.call-update) | async-done | bytes 1572880 | tf_op jit(solution)/shard_map/all_gather | solution.py:30
  137.8 3.8 %fusion.9 = f32[384,576]{1,0:T(8,128)} fusion(bf16[384,2048]{1,0:T(8,128)(2,1)} %all-gather.2.cloned.1.call-done, bf16[2048,576]{0,1:T(8,128)(2,1)S(1)} %copy-done), kind=kOutput, calls=%fused_computation.14 | convolution fusion | flops 905969664 | bytes 4816896 | tf_op jit(solution)/shard_map/dot_general | solution.py:34
  141.6 3.5 %all-to-all-start.1 = ((f32[4,96,576]{2,1,0:T(8,128)}), f32[4,96,576]{2,1,0:T(8,128)S(1)}, u32[]{:S(2)}, u32[]{:S(2)}) async-start(f32[4,96,576]{2,1,0:T(8,128)} %bitcast.17), calls=%async_computation.2 | async-start | bytes 1966080 | tf_op jit(solution)/shard_map/all_to_all | solution.py:35
  146.3 11.2 %all-to-all-done.1 = f32[4,96,576]{2,1,0:T(8,128)S(1)} async-done(((f32[4,96,576]{2,1,0:T(8,128)}), f32[4,96,576]{2,1,0:T(8,128)S(1)}, u32[]{:S(2)}, u32[]{:S(2)}) %all-to-all-start.1) | async-done | bytes 884768 | tf_op jit(solution)/shard_map/all_to_all | solution.py:35
  157.5 0.9 copy-done.4
  158.4 2.8 %copy.13 = f32[96,4,576]{2,1,0:T(4,128)} copy(f32[96,4,576]{2,0,1:T(8,128)} %bitcast.16) | data formatting | bytes 1769472 | tf_op jit(solution)/shard_map/all_to_all | solution.py:35
  161.3 2.7 %all_to_all.35 = f32[96,2304]{1,0:T(8,128)} reshape(f32[96,4,576]{2,1,0:T(4,128)} %copy.13) | data formatting | bytes 1769472 | tf_op jit(solution)/shard_map/all_to_all | solution.py:35
  164.0 32.7 %fusion = f32[16,2304]{1,0:T(8,128)S(1)} fusion(f32[96,2304]{1,0:T(8,128)} %all_to_all.35), kind=kCustom, calls=%all-reduce-scatter | all-reduce-scatter fusion | flops 294913 | bytes 1032704
  196.7 1.9 collective-permute-start
  198.6 2.4 %collective-permute-start.1 = (f32[12,2304]{1,0:T(8,128)S(1)}, f32[12,2304]{1,0:T(8,128)S(1)}, u32[]{:S(2)}, u32[]{:S(2)}) collective-permute-start(f32[12,2304]{1,0:T(8,128)S(1)} %slice), channel_id=1, source_target_pairs={{0,2},{1,3},{2,4},{3,5},{4,6},{5,7},{8,10},{9,11},{10,12},{11,13},... | collective-permute-start | bytes 331784
  201.0 5.0 %fusion.8 = f32[2048,576]{0,1:T(8,128)} fusion(bf16[384,2048]{1,0:T(8,128)(2,1)} %all-gather.2.cloned.1.call-done, bf16[384,576]{1,0:T(8,128)(2,1)S(1)} %bitcast.15), kind=kOutput, calls=%fused_computation.13 | convolution fusion | flops 905969664 | bytes 6733824 | tf_op jit(solution)/shard_map/dot_general | solution.py:31
  206.1 2.0 collective-permute-done.1
  208.5 0.7 constant_dynamic-slice_fusion
  (24 shorter events, 3.2 us)
Async XLA Ops:
  7.2 15.5 %copy-start = (bf16[2048,576]{0,1:T(8,128)(2,1)S(1)}, bf16[2048,576]{0,1:T(8,128)(2,1)}, u32[]{:S(2)}) copy-start(bf16[2048,576]{0,1:T(8,128)(2,1)} %param.4) | copy-start | bytes 7077892
  7.2 63.5 %reduce-scatter.4.cloned.1.call-start = ((), (), s32[]{:S(2)}) async-start(), calls=%async_computation.3 | async-start | bytes 3932160 | tf_op jit(solution)/shard_map/reduce_scatter | solution.py:12
  21.8 0.8 copy-start.2
  25.7 1.0 copy-start.5
  25.7 112.1 %all-gather.2.cloned.1.call-start = ((), (), s32[]{:S(2)}) async-start(), calls=%async_computation.4 | async-start | bytes 1966080 | tf_op jit(solution)/shard_map/all_gather | solution.py:30
  70.6 36.2 %copy-start.1 = (f32[96,2048]{1,0:T(8,128)S(1)}, f32[96,2048]{1,0:T(8,128)}, u32[]{:S(2)}) copy-start(f32[96,2048]{1,0:T(8,128)} %reduce-scatter.4.cloned.1.call-done) | copy-start | bytes 2359300
  108.0 37.1 %copy-start.6 = (u32[32]{0:T(128)S(1)}, u32[32]{0:T(128)}, u32[]{:S(2)}) copy-start(u32[32]{0:T(128)} %constant.10) | copy-start | bytes 388
  141.6 15.9 %all-to-all-start.1 = ((f32[4,96,576]{2,1,0:T(8,128)}), f32[4,96,576]{2,1,0:T(8,128)S(1)}, u32[]{:S(2)}, u32[]{:S(2)}) async-start(f32[4,96,576]{2,1,0:T(8,128)} %bitcast.17), calls=%async_computation.2 | async-start | bytes 1966080 | tf_op jit(solution)/shard_map/all_to_all | solution.py:35
  157.5 0.9 copy-start.4
  158.4 42.6 %copy-start.3 = (bf16[96,4,576]{2,0,1:T(8,128)(2,1)S(1)}, bf16[96,4,576]{2,0,1:T(8,128)(2,1)}, u32[]{:S(2)}) copy-start(bf16[96,4,576]{2,0,1:T(8,128)(2,1)} %copy-done.2) | copy-start | bytes 1327108
  196.7 11.4 %collective-permute-start = (f32[16,2304]{1,0:T(8,128)S(1)}, f32[16,2304]{1,0:T(8,128)S(1)}, u32[]{:S(2)}, u32[]{:S(2)}) collective-permute-start(f32[16,2304]{1,0:T(8,128)S(1)} %fusion), channel_id=1, source_target_pairs={{0,1},{1,2},{2,3},{3,4},{4,5},{5,6},{6,7},{8,9},{9,10},{10,11},{11... | collective-permute-start | bytes 442376
  198.6 9.5 %collective-permute-start.1 = (f32[12,2304]{1,0:T(8,128)S(1)}, f32[12,2304]{1,0:T(8,128)S(1)}, u32[]{:S(2)}, u32[]{:S(2)}) collective-permute-start(f32[12,2304]{1,0:T(8,128)S(1)} %slice), channel_id=1, source_target_pairs={{0,2},{1,3},{2,4},{3,5},{4,6},{5,7},{8,10},{9,11},{10,12},{11,13},... | collective-permute-start | bytes 331784
Sparse Core Ops, SparseCore 0:
  25.8 44.7 reduce-scatter.3
  108.1 29.6 all-gather.1
where the time goes:
time: 217 us; the launch traced here: 216 us
  waiting for transfers between devices  86.8 us (40%)
  blocking collectives  78.7 us (36%)
  between operations  14.8 us (7%)
  matrix products  11.9 us (5%)
  local copies, waits for them, and re-layouts  10.5 us (5%)
  starting transfers between devices  7.91 us (4%)
  other arithmetic  5.41 us (2%)
    reduce_scatter x1, waiting for transfers between devices, local(): lax.psum_scatter(lax.dot_general(width_part, embedding, (((1,), (1,)), ((...  43.8 us
    unnamed x1, blocking collectives  32.7 us
    all_gather x1, waiting for transfers between devices, local(): grad_piece = lax.all_gather(grads, 'layer', axis=0, tiled=True)  29.8 us
    pmax x1, blocking collectives, local(): lax.pmax((jnp.max(logits, axis=1), jnp.max(teach_f, axis=1)), ('row', 'co...  17.8 us
    psum x1, blocking collectives, local(): sum_s, sum_t = lax.psum((part_s, part_t), ('row', 'col'))  14.2 us
    all_to_all x1, blocking collectives, local(): lax.all_to_all(token_rows, 'layer', split_axis=1, concat_axis=0, tiled=True)  11.5 us
    all_to_all x1, waiting for transfers between devices, local(): lax.all_to_all(hidden_piece, 'layer', split_axis=0, concat_axis=1, tiled=...  11.2 us
    all_to_all x2, local copies, waits for them, and re-layouts, local(): lax.all_to_all(hidden_piece, 'layer', split_axis=0, concat_axis=1, tiled=...  5.53 us
  transfers between devices with their start and end apart: 5, of which 4 were waited for; matrix products, arithmetic and copies ran while one was open for 3% of the time, Pallas kernels for 0%

commit v1 on v0

--- a/solution.py
+++ b/solution.py
@@ -27,7 +27,14 @@
     prob_s = jnp.exp(logits - lse_s[:, None])
     prob_t = jnp.exp(teach_f - lse_t[:, None])
     grads = ((prob_s - prob_t) * LOSS_SCALE).astype(jnp.bfloat16)
-    grad_piece = lax.all_gather(grads, "layer", axis=0, tiled=True)
+    ring = [grads]
+    for hop in range(3):
+        ring.append(lax.ppermute(ring[-1], "layer", [(dev, (dev + 1) % 4) for dev in range(4)]))
+    grad_piece = jnp.roll(
+        jnp.concatenate(ring[::-1], axis=0),
+        (lax.axis_index("layer") + 1) * ring[0].shape[0],
+        axis=0,
+    )
     embed_acc = lax.dot_general(
         grad_piece, width_part, (((0,), (0,)), ((), ())), preferred_element_type=jnp.float32
     )

time: 217 us -> 221 us (1.018)
  waiting for transfers between devices: 86.8 us -> 90.7 us
  local copies, waits for them, and re-layouts: 10.5 us -> 13.8 us
  blocking collectives: 78.7 us -> 76.2 us
    ppermute x0 -> x3, waiting for transfers between devices: none -> 32.1 us  [local(): lax.ppermute(ring[-1], 'layer', [(dev, (dev + 1) % 4) for dev in range(4)])]
    all_gather x1 -> x0, waiting for transfers between devices: 29.8 us -> none  [local(): grad_piece = lax.all_gather(grads, 'layer', axis=0, tiled=True)]
    unnamed x18 -> x23, local copies, waits for them, and re-layouts: 4.34 us -> 7.61 us
  transfers between devices with their start and end apart: 5 -> 7, of which waited for: 4 -> 6; matrix products, arithmetic and copies ran while one was open for 3% -> 3% of each run, Pallas kernels for 0% -> 0%
where the time goes in v1:
time: 221 us; the launch traced here: 220 us
  waiting for transfers between devices  90.7 us (41%)
  blocking collectives  76.2 us (34%)
  between operations  14.9 us (7%)
  local copies, waits for them, and re-layouts  13.8 us (6%)
  matrix products  10.5 us (5%)
  starting transfers between devices  9.63 us (4%)
  other arithmetic  4.54 us (2%)
    reduce_scatter x1, waiting for transfers between devices, local(): lax.psum_scatter(lax.dot_general(width_part, embedding, (((1,), (1,)), ((...  44.8 us
    ppermute x3, waiting for transfers between devices, local(): lax.ppermute(ring[-1], 'layer', [(dev, (dev + 1) % 4) for dev in range(4)])  32.1 us
    unnamed x1, blocking collectives  30.7 us
    pmax x1, blocking collectives, local(): lax.pmax((jnp.max(logits, axis=1), jnp.max(teach_f, axis=1)), ('row', 'co...  17.8 us
    psum x1, blocking collectives, local(): sum_s, sum_t = lax.psum((part_s, part_t), ('row', 'col'))  13.7 us
    all_to_all x1, blocking collectives, local(): lax.all_to_all(token_rows, 'layer', split_axis=1, concat_axis=0, tiled=True)  11.5 us
    all_to_all x1, waiting for transfers between devices, local(): lax.all_to_all(hidden_piece, 'layer', split_axis=0, concat_axis=1, tiled=...  11.3 us
    unnamed x23, local copies, waits for them, and re-layouts  7.61 us
  transfers between devices with their start and end apart: 7, of which 6 were waited for; matrix products, arithmetic and copies ran while one was open for 3% of the time, Pallas kernels for 0%

profile of v1, /device:TPU:1, one launch (start us, length us, event | category | flops | bytes accessed | tf_op | source)
XLA Modules:
  0.0 220.2 jit_solution(13972123578201793514)
XLA Ops:
  7.2 2.5 %all_gather.3 = bf16[96,2304]{1,0:T(8,128)(2,1)S(1)} all-gather(bf16[48,2304]{1,0:T(8,128)(2,1)} %param.3), channel_id=1, replica_groups=mesh['layer'=4,'row'=2,'col'=4] {'row'}, dimensions={0}, use_global_device_ids=true | all-gather | bytes 663552 | tf_op jit(solution)/shard_map/all_gather | solution.py:10
  10.3 11.5 %all_to_all.38 = bf16[96,4,576]{2,0,1:T(8,128)(2,1)S(1)} all-to-all(bf16[96,4,576]{2,0,1:T(8,128)(2,1)S(1)} %copy.11), channel_id=1, replica_groups=mesh['layer'=4,'row'=2,'col'=4] {'layer'}, dimensions={1} | all-to-all | bytes 884736 | tf_op jit(solution)/shard_map/all_to_all | solution.py:11
  21.8 3.1 %fusion.13 = f32[384,2048]{1,0:T(8,128)} fusion(bf16[384,576]{1,0:T(8,128)(2,1)S(1)} %bitcast.12, bf16[2048,576]{0,1:T(8,128)(2,1)S(1)} %copy-done), kind=kOutput, calls=%fused_computation.26 | convolution fusion | flops 905969664 | bytes 5947392 | tf_op jit(solution)/shard_map/dot_general | solution.py:13
  25.1 44.8 %reduce-scatter.4.cloned.1.call-done = f32[96,2048]{1,0:T(8,128)} async-done(((f32[384,2048]{1,0:T(8,128)}), f32[96,2048]{1,0:T(8,128)}) %reduce-scatter.4.cloned.1.call-update) | async-done | bytes 786448 | tf_op jit(solution)/shard_map/reduce_scatter | solution.py:12
  69.8 1.3 reduce_max.23
  71.1 17.8 %all-reduce.3 = (f32[96]{0:T(128)S(1)}, f32[96]{0:T(128)S(1)}) all-reduce(bf16[96]{0:T(256)(128)(2,1)S(1)} %reduce_max.24, f32[96]{0:T(128)S(1)} %reduce_max.23), channel_id=1, replica_groups=mesh['layer'=4,'row'=2,'col'=4] {'row','col'}, use_global_device_ids=true, to_apply=%region_6.0 | all-reduce | flops 192 | bytes 1344 | tf_op jit(solution)/shard_map/pmax | solution.py:21
  88.9 1.5 fusion.6
  90.5 13.7 %all-reduce.2 = (f32[96]{0:T(128)S(1)}, f32[96]{0:T(128)S(1)}) all-reduce(f32[96]{0:T(128)S(1)} %get-tuple-element.6, f32[96]{0:T(128)S(1)} %get-tuple-element.7), channel_id=1, replica_groups=mesh['layer'=4,'row'=2,'col'=4] {'row','col'}, use_global_device_ids=true, to_apply=%region_8.0 | all-reduce | flops 192 | bytes 1536 | tf_op jit(solution)/shard_map/psum | solution.py:24
  104.2 1.6 fusion.10
  105.8 1.2 collective-permute-start
  107.0 10.7 %collective-permute-done = bf16[96,2048]{1,0:T(8,128)(2,1)S(1)} collective-permute-done((bf16[96,2048]{1,0:T(8,128)(2,1)S(1)}, bf16[96,2048]{1,0:T(8,128)(2,1)S(1)}, u32[]{:S(2)}, u32[]{:S(2)}) %collective-permute-start) | collective-permute-done | bytes 393248 | tf_op jit(solution)/shard_map/ppermute | solution.py:32
  118.8 10.9 %collective-permute-done.1 = bf16[96,2048]{1,0:T(8,128)(2,1)} collective-permute-done((bf16[96,2048]{1,0:T(8,128)(2,1)S(1)}, bf16[96,2048]{1,0:T(8,128)(2,1)}, u32[]{:S(2)}, u32[]{:S(2)}) %collective-permute-start.1) | collective-permute-done | bytes 393248 | tf_op jit(solution)/shard_map/ppermute | solution.py:32
  129.6 10.5 %collective-permute-done.2 = bf16[96,2048]{1,0:T(8,128)(2,1)} collective-permute-done((bf16[96,2048]{1,0:T(8,128)(2,1)}, bf16[96,2048]{1,0:T(8,128)(2,1)}, u32[]{:S(2)}, u32[]{:S(2)}) %collective-permute-start.2) | collective-permute-done | bytes 393248 | tf_op jit(solution)/shard_map/ppermute | solution.py:32
  142.2 1.0 constant_dynamic-update-slice_fusion.5
  145.4 2.4 %fusion.1 = f32[384,576]{1,0:T(8,128)} fusion(bf16[2048,576]{0,1:T(8,128)(2,1)S(1)} %copy-done, bf16[768,2048]{1,0:T(8,128)(2,1)S(1)} %constant_dynamic-update-slice_fusion, s32[]{:T(128)S(6)} %select_n.14), kind=kOutput, calls=%fused_computation | convolution fusion | flops 905969664 | bytes 4816900 | tf_op jit(solution)/shard_map/dot_general | solution.py:41
  147.8 4.2 %all-to-all-start.1 = ((f32[4,96,576]{2,1,0:T(8,128)}), f32[4,96,576]{2,1,0:T(8,128)}, u32[]{:S(2)}, u32[]{:S(2)}) async-start(f32[4,96,576]{2,1,0:T(8,128)} %bitcast.14), calls=%async_computation.2 | async-start | bytes 1966080 | tf_op jit(solution)/shard_map/all_to_all | solution.py:42
  153.3 11.3 %all-to-all-done.1 = f32[4,96,576]{2,1,0:T(8,128)} async-done(((f32[4,96,576]{2,1,0:T(8,128)}), f32[4,96,576]{2,1,0:T(8,128)}, u32[]{:S(2)}, u32[]{:S(2)}) %all-to-all-start.1) | async-done | bytes 884768 | tf_op jit(solution)/shard_map/all_to_all | solution.py:42
  164.6 2.8 %copy.13 = f32[96,4,576]{2,1,0:T(4,128)} copy(f32[96,4,576]{2,0,1:T(8,128)} %bitcast.3) | data formatting | bytes 1769472 | tf_op jit(solution)/shard_map/all_to_all | solution.py:42
  167.3 2.7 %all_to_all.35 = f32[96,2304]{1,0:T(8,128)} reshape(f32[96,4,576]{2,1,0:T(4,128)} %copy.13) | data formatting | bytes 1769472 | tf_op jit(solution)/shard_map/all_to_all | solution.py:42
  170.1 30.7 %fusion = f32[16,2304]{1,0:T(8,128)S(1)} fusion(f32[96,2304]{1,0:T(8,128)} %all_to_all.35), kind=kCustom, calls=%all-reduce-scatter | all-reduce-scatter fusion | flops 294913 | bytes 1032704
  200.8 1.9 collective-permute-start.3
  202.8 1.9 collective-permute-start.4
  204.7 5.0 %fusion.3 = f32[2048,576]{0,1:T(8,128)} fusion(bf16[384,576]{1,0:T(8,128)(2,1)S(1)} %bitcast.13, bf16[768,2048]{1,0:T(8,128)(2,1)} %copy-done.4, s32[]{:T(128)S(6)} %select_n.14), kind=kOutput, calls=%fused_computation.2 | convolution fusion | flops 905969664 | bytes 6733828 | tf_op jit(solution)/shard_map/dot_general | solution.py:38
  209.7 2.5 %collective-permute-done.4 = f32[12,2304]{1,0:T(8,128)S(1)} collective-permute-done((f32[12,2304]{1,0:T(8,128)S(1)}, f32[12,2304]{1,0:T(8,128)S(1)}, u32[]{:S(2)}, u32[]{:S(2)}) %collective-permute-start.4) | collective-permute-done | bytes 110624
  (33 shorter events, 7.7 us)
Async XLA Ops:
  7.2 14.7 %copy-start = (bf16[2048,576]{0,1:T(8,128)(2,1)S(1)}, bf16[2048,576]{0,1:T(8,128)(2,1)}, u32[]{:S(2)}) copy-start(bf16[2048,576]{0,1:T(8,128)(2,1)} %param.4) | copy-start | bytes 7077892
  7.2 62.7 %reduce-scatter.4.cloned.1.call-start = ((), (), s32[]{:S(2)}) async-start(), calls=%async_computation.3 | async-start | bytes 3932160 | tf_op jit(solution)/shard_map/reduce_scatter | solution.py:12
  21.8 3.1 %copy-start.1 = (bf16[96,2048]{1,0:T(8,128)(2,1)S(1)}, bf16[96,2048]{1,0:T(8,128)(2,1)}, u32[]{:S(2)}) copy-start(bf16[96,2048]{1,0:T(8,128)(2,1)} %param.5) | copy-start | bytes 1179652
  105.8 12.0 %collective-permute-start = (bf16[96,2048]{1,0:T(8,128)(2,1)S(1)}, bf16[96,2048]{1,0:T(8,128)(2,1)S(1)}, u32[]{:S(2)}, u32[]{:S(2)}) collective-permute-start(bf16[96,2048]{1,0:T(8,128)(2,1)S(1)} %fusion.10), channel_id=1, source_target_pairs={{0,8},{8,16},{16,24},{24,0},{1,9},{9,17},{17,25},{25,1},{2,10},{10... | collective-permute-start | bytes 1179656 | tf_op jit(solution)/shard_map/ppermute | solution.py:32
  117.7 0.7 copy-start.2
  118.5 11.2 %collective-permute-start.1 = (bf16[96,2048]{1,0:T(8,128)(2,1)S(1)}, bf16[96,2048]{1,0:T(8,128)(2,1)}, u32[]{:S(2)}, u32[]{:S(2)}) collective-permute-start(bf16[96,2048]{1,0:T(8,128)(2,1)S(1)} %collective-permute-done), channel_id=1, source_target_pairs={{0,8},{8,16},{16,24},{24,0},{1,9},{9,17},{17,25},{25,1},{2,10},{10... | collective-permute-start | bytes 1179656 | tf_op jit(solution)/shard_map/ppermute | solution.py:32
  129.6 10.5 %collective-permute-start.2 = (bf16[96,2048]{1,0:T(8,128)(2,1)}, bf16[96,2048]{1,0:T(8,128)(2,1)}, u32[]{:S(2)}, u32[]{:S(2)}) collective-permute-start(bf16[96,2048]{1,0:T(8,128)(2,1)} %collective-permute-done.1), channel_id=1, source_target_pairs={{0,8},{8,16},{16,24},{24,0},{1,9},{9,17},{17,25},{25,1},{2,10},{10... | collective-permute-start | bytes 1179656 | tf_op jit(solution)/shard_map/ppermute | solution.py:32
  129.6 15.7 %copy-start.3 = (bf16[96,2048]{1,0:T(8,128)(2,1)S(1)}, bf16[96,2048]{1,0:T(8,128)(2,1)}, u32[]{:S(2)}) copy-start(bf16[96,2048]{1,0:T(8,128)(2,1)} %copy-done.2) | copy-start | bytes 1179652
  145.4 2.4 %copy-start.4 = (bf16[768,2048]{1,0:T(8,128)(2,1)}, bf16[768,2048]{1,0:T(8,128)(2,1)S(1)}, u32[]{:S(2)}) copy-start(bf16[768,2048]{1,0:T(8,128)(2,1)S(1)} %constant_dynamic-update-slice_fusion) | copy-start | bytes 9437188
  145.4 6.6 %copy-start.5 = (u32[32]{0:T(128)S(1)}, u32[32]{0:T(128)}, u32[]{:S(2)}) copy-start(u32[32]{0:T(128)} %constant.38) | copy-start | bytes 388
  147.8 16.8 %all-to-all-start.1 = ((f32[4,96,576]{2,1,0:T(8,128)}), f32[4,96,576]{2,1,0:T(8,128)}, u32[]{:S(2)}, u32[]{:S(2)}) async-start(f32[4,96,576]{2,1,0:T(8,128)} %bitcast.14), calls=%async_computation.2 | async-start | bytes 1966080 | tf_op jit(solution)/shard_map/all_to_all | solution.py:42
  200.8 11.4 %collective-permute-start.3 = (f32[16,2304]{1,0:T(8,128)S(1)}, f32[16,2304]{1,0:T(8,128)S(1)}, u32[]{:S(2)}, u32[]{:S(2)}) collective-permute-start(f32[16,2304]{1,0:T(8,128)S(1)} %fusion), channel_id=1, source_target_pairs={{0,1},{1,2},{2,3},{3,4},{4,5},{5,6},{6,7},{8,9},{9,10},{10,11},{11... | collective-permute-start | bytes 442376
  202.8 9.5 %collective-permute-start.4 = (f32[12,2304]{1,0:T(8,128)S(1)}, f32[12,2304]{1,0:T(8,128)S(1)}, u32[]{:S(2)}, u32[]{:S(2)}) collective-permute-start(f32[12,2304]{1,0:T(8,128)S(1)} %slice), channel_id=1, source_target_pairs={{0,2},{1,3},{2,4},{3,5},{4,6},{5,7},{8,10},{9,11},{10,12},{11,13},... | collective-permute-start | bytes 331784
Sparse Core Ops, SparseCore 0:
  25.0 44.7 reduce-scatter.3
